TPU v7x, 256 devices: a whole 4x4x8 slice. The times are simulated.
256 devices in a mesh: row: 16 (over x_lo, y, core), col: 16 (over z, x_hi).
Axes of the slice: x: 4 (x_hi: 2, x_lo: 2; x = x_hi * 2 + x_lo), y: 4, z: 8, core: 2. Of those that a mesh axis runs over, the one named last changes fastest.
Arguments:
- labels: int32 [16, 512, 2048], P(None, 'row', 'col'), may hold values from 0 to 11
- pressure: float32 [16, 512, 2048], P(None, 'row', 'col'), may hold values from -6 to 6
- velocity_x: float32 [16, 512, 2048], P(None, 'row', 'col'), may hold values from -6 to 6
- velocity_y: float32 [16, 512, 2048], P(None, 'row', 'col'), may hold values from -6 to 6
- velocity_z: float32 [16, 512, 2048], P(None, 'row', 'col'), may hold values from -6 to 6
- speed_table: float32 [12], replicated, may hold values from 0.8 to 2
- density_table: float32 [12], replicated, may hold values from 0.9 to 1.9
- filter_taps: float32 [33], replicated, may hold values from -0.2 to 0.8, as said below
- layer_width: int32 [4], replicated, may hold values from 10 to 40
Outputs:
- pressure_next: float32 [16, 512, 2048], P(None, 'row', 'col')
- velocity_x_next: float32 [16, 512, 2048], P(None, 'row', 'col')
- velocity_y_next: float32 [16, 512, 2048], P(None, 'row', 'col')
- velocity_z_next: float32 [16, 512, 2048], P(None, 'row', 'col')
Inputs may be any that keep to these rules, and one draw needn't show every extreme that they name: `filter_taps`: tap k weighs the cell k - 16 positions away.
All inputs are finite; a program needn't handle non-finite values.
Results may differ from a plain program's by a relative error of at most 0.000068.
Values sent between devices are 32-bit elements; how exact they have to be, the bound alone decides.
A program may use at most 64 MiB of HBM per device.

v0:
```python
import math
import jax
import jax.numpy as jnp
from jax import lax
from jax.sharding import PartitionSpec as P

time_step = 0.15
reference_speed = 2.0
absorption = 6.0
highest = lax.Precision.HIGHEST


def extended(array, sides, width):
    for axis, dim in sides:
        size, length = (lax.axis_size(axis), array.shape[dim])
        up = [(i, (i + 1) % size) for i in range(size)]
        down = [(j, i) for i, j in up]
        last = lax.slice_in_dim(array, length - width, length, axis=dim)
        initial = lax.slice_in_dim(array, 0, width, axis=dim)
        before = lax.ppermute(last, axis, up)
        after = lax.ppermute(initial, axis, down)
        array = jnp.concatenate([before, array, after], axis=dim)
    return array


def factor_pair(length):
    leading = math.gcd(length, 2 ** ((length.bit_length() - 1) // 2))
    return (leading, length // leading)


def angle_table(height, breadth, length, phase_sign):
    product = (
        jnp.arange(height, dtype=jnp.int32)[:, None]
        * jnp.arange(breadth, dtype=jnp.int32)[None, :]
        % length
    )
    angles = product.astype(jnp.float32) * (2.0 * math.pi / length)
    return (jnp.cos(angles), phase_sign * jnp.sin(angles))


def complex_contract(pieces, tables, form):
    real_part, imag_part = pieces
    cosines, sine_part = tables

    def product(operand, matrix):
        return jnp.einsum(form, operand, matrix, precision=highest)

    return (
        product(real_part, cosines) - product(imag_part, sine_part),
        product(real_part, sine_part) + product(imag_part, cosines),
    )


def complex_times(factor, pieces):
    return (
        factor[0] * pieces[0] - factor[1] * pieces[1],
        factor[0] * pieces[1] + factor[1] * pieces[0],
    )


def line_transform(pieces, on_last, inverse):
    real_part, imag_part = pieces
    position = real_part.ndim - 1 if on_last else real_part.ndim - 2
    length = real_part.shape[position]
    leading, trailing = factor_pair(length)
    phase_sign = 1.0 if inverse else -1.0
    new_shape = real_part.shape[:position] + (leading, trailing) + real_part.shape[position + 1 :]
    pieces = (real_part.reshape(new_shape), imag_part.reshape(new_shape))
    outer_table = angle_table(leading, leading, leading, phase_sign)
    inner_table = angle_table(trailing, trailing, trailing, phase_sign)
    twiddle = angle_table(leading, trailing, length, phase_sign)
    suffix = ""
    if not on_last:
        twiddle = (twiddle[0][:, :, None], twiddle[1][:, :, None])
        suffix = "x"
    if inverse:
        pieces = complex_contract(pieces, inner_table, "...kl" + suffix + ",lb->...kb" + suffix)
        pieces = complex_times(twiddle, pieces)
        pieces = complex_contract(pieces, outer_table, "...kb" + suffix + ",ka->...ab" + suffix)
        factor = 1.0 / length
        pieces = (pieces[0] * factor, pieces[1] * factor)
    else:
        pieces = complex_contract(pieces, outer_table, "...ab" + suffix + ",ak->...kb" + suffix)
        pieces = complex_times(twiddle, pieces)
        pieces = complex_contract(pieces, inner_table, "...kb" + suffix + ",bl->...kl" + suffix)
    initial = real_part.shape
    return (pieces[0].reshape(initial), pieces[1].reshape(initial))


def transform_x(pieces):
    return line_transform(pieces, True, False)


def transform_y(pieces):
    return line_transform(pieces, False, False)


def untransform_x(pieces):
    return line_transform(pieces, True, True)


def untransform_y(pieces):
    return line_transform(pieces, False, True)


def depth_forward(pieces):
    length = pieces[0].shape[1]
    return complex_contract(pieces, angle_table(length, length, length, -1.0), "fzyx,zk->fkyx")


def depth_inverse(pieces):
    length = pieces[0].shape[1]
    result = complex_contract(pieces, angle_table(length, length, length, 1.0), "fkyx,kz->fzyx")
    factor = 1.0 / length
    return (result[0] * factor, result[1] * factor)


def packed(operation, stacked):
    result = operation((stacked[0], stacked[1]))
    return jnp.stack([result[0], result[1]])


def natural_wave(indices, length):
    signed = jnp.where(indices < length // 2, indices, indices - length)
    return signed.astype(jnp.float32) * (2.0 * math.pi / length)


def ordered_wave(position, length):
    leading, trailing = factor_pair(length)
    return natural_wave(position // trailing + leading * (position % trailing), length)


def forward_rows(pieces):
    pieces = depth_forward(pieces)
    stacked = jnp.stack([pieces[0], pieces[1]])
    stacked = packed(
        transform_y, lax.all_to_all(stacked, "row", split_axis=2, concat_axis=3, tiled=True)
    )
    stacked = packed(
        transform_x, lax.all_to_all(stacked, "col", split_axis=3, concat_axis=4, tiled=True)
    )
    return (stacked[0], stacked[1])


def inverse_rows(pieces):
    pieces = untransform_x(pieces)
    stacked = jnp.stack([pieces[0], pieces[1]])
    stacked = packed(
        untransform_y, lax.all_to_all(stacked, "col", split_axis=4, concat_axis=3, tiled=True)
    )
    stacked = packed(
        depth_inverse, lax.all_to_all(stacked, "row", split_axis=3, concat_axis=2, tiled=True)
    )
    return (stacked[0], stacked[1])


def waves_rows(spectral_shape):
    planes, height, breadth = (spectral_shape[1], spectral_shape[2], spectral_shape[3])
    depth_ids = lax.axis_index("row") * planes + jnp.arange(planes, dtype=jnp.int32)
    cross_ids = lax.axis_index("col") * height + jnp.arange(height, dtype=jnp.int32)
    wave_z = natural_wave(depth_ids, planes * lax.axis_size("row"))[:, None, None]
    wave_y = ordered_wave(cross_ids, height * lax.axis_size("col"))[None, :, None]
    wave_x = ordered_wave(jnp.arange(breadth, dtype=jnp.int32), breadth)[None, None, :]
    return (wave_z, wave_y, wave_x)


def derivative(wavenum, correction, phase_sign):
    half_wave = 0.5 * wavenum
    return (
        phase_sign * wavenum * jnp.sin(half_wave) * correction,
        wavenum * jnp.cos(half_wave) * correction,
    )


def band_matrix(filter_taps, extent):
    tap_count = filter_taps.shape[0]
    offset = (
        jnp.arange(extent + tap_count - 1, dtype=jnp.int32)[:, None]
        - jnp.arange(extent, dtype=jnp.int32)[None, :]
    )
    selected = offset[:, :, None] == jnp.arange(tap_count, dtype=jnp.int32)[None, None, :]
    return jnp.sum(jnp.where(selected, filter_taps[None, None, :], 0.0), axis=2)


def absorber(position, length, low_width, high_width):
    low_part = jnp.maximum(low_width - position, 0).astype(jnp.float32) / low_width.astype(
        jnp.float32
    )
    high_part = jnp.maximum(position - (length - 1 - high_width), 0).astype(
        jnp.float32
    ) / high_width.astype(jnp.float32)
    damping = absorption * reference_speed * (low_part**4 + high_part**4)
    return jnp.exp(-0.5 * time_step * damping)


def spectral_correction(wave_z, wave_y, wave_x):
    return jnp.sinc(
        reference_speed
        * time_step
        * jnp.sqrt(wave_x * wave_x + wave_y * wave_y + wave_z * wave_z)
        / (2.0 * math.pi)
    )


def on_device(
    labels,
    pressure,
    velocity_x,
    velocity_y,
    velocity_z,
    speed_table,
    density_table,
    filter_taps,
    layer_width,
):
    planes, height, breadth = pressure.shape
    buoyancy_of = 1.0 / density_table
    modulus_of = density_table * speed_table * speed_table
    buoyancy = jnp.zeros(pressure.shape, jnp.float32)
    modulus = jnp.zeros(pressure.shape, jnp.float32)
    for label_id in range(speed_table.shape[0]):
        matches = labels == label_id
        buoyancy = jnp.where(matches, buoyancy_of[label_id], buoyancy)
        modulus = jnp.where(matches, modulus_of[label_id], modulus)
    coefficients = jnp.stack([buoyancy, modulus])
    reach = filter_taps.shape[0] // 2
    across = band_matrix(filter_taps, breadth)
    downward = band_matrix(filter_taps, height)
    padded = extended(coefficients, (("col", 3),), reach)
    smoothed = jnp.einsum("fzyj,ji->fzyi", padded, across, precision=highest)
    padded = extended(smoothed, (("row", 2),), reach)
    smoothed = jnp.einsum("fzjx,jy->fzyx", padded, downward, precision=highest)
    buoyancy = smoothed[0]
    modulus = smoothed[1]
    column_ids = lax.axis_index("col") * breadth + jnp.arange(breadth, dtype=jnp.int32)
    row_ids = lax.axis_index("row") * height + jnp.arange(height, dtype=jnp.int32)
    damp_x = absorber(column_ids, breadth * lax.axis_size("col"), layer_width[0], layer_width[1])[
        None, None, :
    ]
    damp_y = absorber(row_ids, height * lax.axis_size("row"), layer_width[2], layer_width[3])[
        None, :, None
    ]
    empty = jnp.zeros(pressure.shape, jnp.float32)
    forward, inverse, waves_of = (forward_rows, inverse_rows, waves_rows)
    pressure_hat = forward((pressure[None], empty[None]))
    wave_z, wave_y, wave_x = waves_of(pressure_hat[0].shape)
    correction = spectral_correction(wave_z, wave_y, wave_x)
    pressure_one = (pressure_hat[0][0], pressure_hat[1][0])
    grad_x_hat = complex_times(derivative(wave_x, correction, -1.0), pressure_one)
    grad_y_hat = complex_times(derivative(wave_y, correction, -1.0), pressure_one)
    grad_z_hat = complex_times(derivative(wave_z, correction, -1.0), pressure_one)
    packed_real = jnp.stack([grad_x_hat[0] - grad_y_hat[1], grad_z_hat[0]])
    packed_imag = jnp.stack([grad_x_hat[1] + grad_y_hat[0], grad_z_hat[1]])
    gradients = inverse((packed_real, packed_imag))
    grad_x = gradients[0][0]
    grad_y = gradients[1][0]
    grad_z = gradients[0][1]
    next_x = damp_x * (damp_x * velocity_x - time_step * buoyancy * grad_x)
    next_y = damp_y * (damp_y * velocity_y - time_step * buoyancy * grad_y)
    next_z = velocity_z - time_step * buoyancy * grad_z
    velocity_hat = forward((jnp.stack([next_x, next_z]), jnp.stack([next_y, empty])))
    horizontal = (velocity_hat[0][0], velocity_hat[1][0])
    vertical = (velocity_hat[0][1], velocity_hat[1][1])
    flow_x = complex_times(derivative(wave_x, correction, 1.0), horizontal)
    flow_y = complex_times(derivative(wave_y, correction, 1.0), horizontal)
    flow_z = complex_times(derivative(wave_z, correction, 1.0), vertical)
    summed_real = flow_x[0] + flow_y[1] + flow_z[0]
    summed_imag = flow_x[1] - flow_y[0] + flow_z[1]
    divergence = inverse((summed_real[None], summed_imag[None]))[0][0]
    damp_both = damp_x * damp_y
    pressure_next = damp_both * (damp_both * pressure - time_step * modulus * divergence)
    return (pressure_next, next_x, next_y, next_z)


def solution(mesh):
    return jax.shard_map(
        on_device,
        mesh=mesh,
        in_specs=(
            P(None, "row", "col"),
            P(None, "row", "col"),
            P(None, "row", "col"),
            P(None, "row", "col"),
            P(None, "row", "col"),
            P(),
            P(),
            P(),
            P(),
        ),
        out_specs=(
            P(None, "row", "col"),
            P(None, "row", "col"),
            P(None, "row", "col"),
            P(None, "row", "col"),
        ),
        check_vma=False,
    )
```

profile of v0, /device:TPU:1, one launch (start us, length us, event | category | flops | bytes accessed | tf_op | source)
XLA Modules:
  0.0 320.3 jit_solution(11069281004676494393)
XLA Ops:
  5.2 6.9 %all-to-all-start = ((f32[2,1,16,32,128]{4,3,1,0,2:T(8,128)}), f32[2,1,16,32,128]{4,3,1,0,2:T(8,128)S(1)}, u32[]{:S(2)}, u32[]{:S(2)}) async-start(f32[2,1,16,32,128]{4,3,1,0,2:T(8,128)} %copy.316), calls=%async_computation | async-start | bytes 1048576 | tf_op jit(solution)/shard_map/all_to_all | solution.py:137
  12.4 9.4 %all-to-all-done = f32[2,1,16,32,128]{4,3,1,0,2:T(8,128)S(1)} async-done(((f32[2,1,16,32,128]{4,3,1,0,2:T(8,128)}), f32[2,1,16,32,128]{4,3,1,0,2:T(8,128)S(1)}, u32[]{:S(2)}, u32[]{:S(2)}) %all-to-all-start) | async-done | bytes 524320 | tf_op jit(solution)/shard_map/all_to_all | solution.py:137
  27.1 10.6 %all-to-all-start.1 = ((f32[2,1,1,512,128]{4,2,1,0,3:T(1,128)}), f32[2,1,1,512,128]{4,2,1,0,3:T(1,128)S(1)}, u32[]{:S(2)}, u32[]{:S(2)}) async-start(f32[2,1,1,512,128]{4,2,1,0,3:T(1,128)} %pad_maximum_fusion.6), calls=%async_computation.1 | async-start | bytes 1048576 | tf_op jit(solution)/shard_map/all_to_all | solution.py:140
  39.0 15.4 %all-to-all-done.1 = f32[2,1,1,512,128]{4,2,1,0,3:T(1,128)S(1)} async-done(((f32[2,1,1,512,128]{4,2,1,0,3:T(1,128)}), f32[2,1,1,512,128]{4,2,1,0,3:T(1,128)S(1)}, u32[]{:S(2)}, u32[]{:S(2)}) %all-to-all-start.1) | async-done | bytes 524320 | tf_op jit(solution)/shard_map/all_to_all | solution.py:140
  59.9 1.8 add_bitcast_fusion.3
  68.7 2.1 fusion.5
  70.8 3.9 %copy.390 = f32[2,1,32,32,64]{2,0,4,3,1:T(2,128)} copy(f32[2,1,32,32,64]{4,3,2,0,1:T(8,128)} %fusion.5) | data formatting | bytes 1048576 | tf_op jit(solution)/shard_map/stack;reshape | solution.py:147
  74.7 2.1 fusion.3
  76.8 4.1 %copy.391 = f32[2,1,32,32,64]{2,0,4,3,1:T(2,128)} copy(f32[2,1,32,32,64]{4,3,2,0,1:T(8,128)} %fusion.3) | data formatting | bytes 1048576 | tf_op jit(solution)/shard_map/stack;reshape | solution.py:147
  80.9 5.2 %fusion.760 = f32[2048,2,1,2,32]{4,3,2,1,0:T(2,128)} fusion(f32[1,2,1,32,2048]{3,1,2,0,4:T(2,128)} %bitcast.572, f32[1,2,1,32,2048]{3,1,2,0,4:T(2,128)S(1)} %bitcast.571), kind=kLoop, calls=%fused_computation.852 | loop fusion | flops 262144 | bytes 2097152
  86.1 6.6 %reshape.1299 = f32[16,1,16384]{2,1,0:T(1,128)} reshape(f32[2048,2,1,2,32]{4,3,2,1,0:T(2,128)} %fusion.760) | data formatting | bytes 2097152
  92.7 4.5 %all-to-all-start.2 = ((f32[16,1,16384]{2,1,0:T(1,128)}), f32[16,1,16384]{2,1,0:T(1,128)S(1)}, u32[]{:S(2)}, u32[]{:S(2)}) async-start(f32[16,1,16384]{2,1,0:T(1,128)} %reshape.1299), calls=%async_computation.2 | async-start | bytes 2097152 | tf_op jit(solution)/shard_map/all_to_all | solution.py:149
  98.6 8.1 %select_bitcast_fusion.1 = (f32[1,16,32,128]{3,2,1,0:T(8,128)S(1)}, pred[16,32,128]{2,1,0:T(8,128)(4,1)S(1)}, pred[16,32,128]{2,1,0:T(8,128)(4,1)S(1)}, pred[16,...) fusion(f32[]{:T(128)} %bitcast.19, f32[]{:T(128)} %bitcast.18, ...), kind=kLoop, calls=%fused_computation.230 | loop fusion | flops 1572864 | bytes 1310768 | tf_op jit(solution)/shard_map/stack | solution.py:225
  106.7 7.7 %select_bitcast_fusion = f32[1,16,32,128]{3,2,1,0:T(8,128)S(1)} fusion(pred[16,32,128]{2,1,0:T(8,128)(4,1)S(1)} %get-tuple-element.16, pred[16,32,128]{2,1,0:T(8,128)(4,1)S(1)} %get-tuple-element.15, pred[16,32,128]{2,1,0:T(8,128)(4,1)S(1)} %get-tuple-element.14, pred[16,32,128]{2,1,0:T(8,128)(4,1)S(1)} %get-tuple-element.13, ...), kind=kLoop, calls=%fused_computation.229 | loop fusion | flops 786432 | bytes 1048624 | tf_op jit(solution)/shard_map/stack | solution.py:225
  115.4 2.9 collective-permute-start
  118.3 2.2 collective-permute-start.1
  127.2 3.1 reduce
  130.4 5.1 %reshape.1300 = f32[2048,2,1,2,32]{4,3,2,1,0:T(2,128)} reshape(f32[16,16384]{1,0:T(8,128)S(1)} %reduce) | data formatting | bytes 2097152
  135.4 5.2 %copy.330 = f32[2,2,1,32,16,128]{5,3,4,1,2,0:T(8,128)S(1)} copy(f32[2,2,1,32,16,128]{3,1,0,5,4,2:T(2,128)} %bitcast.564) | data formatting | bytes 2097152 | tf_op jit(solution)/shard_map/all_to_all | solution.py:149
  147.3 1.8 copy.337
  149.1 6.5 %all-to-all-start.3 = ((f32[2,2,1,512,128]{4,1,2,0,3:T(2,128)}), f32[2,2,1,512,128]{4,1,2,0,3:T(2,128)S(1)}, u32[]{:S(2)}, u32[]{:S(2)}) async-start(f32[2,2,1,512,128]{4,1,2,0,3:T(2,128)} %copy.337), calls=%async_computation.3 | async-start | bytes 2097152 | tf_op jit(solution)/shard_map/all_to_all | solution.py:152
  155.6 2.3 fusion.28
  161.3 9.6 %collective-permute-done.2 = f32[2,16,16,128]{3,2,1,0:T(8,128)S(1)} collective-permute-done((f32[2,16,16,128]{3,2,1,0:T(8,128)S(1)}, f32[2,16,16,128]{3,2,1,0:T(8,128)S(1)}, u32[]{:S(2)}, u32[]{:S(2)}) %collective-permute-start.2) | collective-permute-done | bytes 262176 | tf_op jit(solution)/shard_map/ppermute | solution.py:20
  181.5 20.8 %all_to_all.96 = f32[2,2,16,32,128]{4,3,1,0,2:T(8,128)S(1)} all-to-all(f32[2,2,16,32,128]{4,3,1,0,2:T(8,128)S(1)} %copy.352), channel_id=1, replica_groups=mesh['row'=16,'col'=16] {'row'}, dimensions={2} | all-to-all | bytes 2097152 | tf_op jit(solution)/shard_map/all_to_all | solution.py:137
  211.3 7.5 %all-to-all-start.5 = ((f32[2,2,1,512,128]{4,1,2,0,3:T(2,128)}), f32[2,2,1,512,128]{4,1,2,0,3:T(2,128)S(1)}, u32[]{:S(2)}, u32[]{:S(2)}) async-start(f32[2,2,1,512,128]{4,1,2,0,3:T(2,128)} %pad_maximum_fusion.3), calls=%async_computation.5 | async-start | bytes 2097152 | tf_op jit(solution)/shard_map/all_to_all | solution.py:140
  218.8 25.9 %all-to-all-done.5 = f32[2,2,1,512,128]{4,1,2,0,3:T(2,128)S(1)} async-done(((f32[2,2,1,512,128]{4,1,2,0,3:T(2,128)}), f32[2,2,1,512,128]{4,1,2,0,3:T(2,128)S(1)}, u32[]{:S(2)}, u32[]{:S(2)}) %all-to-all-start.5) | async-done | bytes 1048608 | tf_op jit(solution)/shard_map/all_to_all | solution.py:140
  265.2 2.0 reshape.1301
  267.2 24.5 %all_to_all.97 = f32[16,1,8192]{2,1,0:T(1,128)S(1)} all-to-all(f32[16,1,8192]{2,1,0:T(1,128)S(1)} %reshape.1301), channel_id=1, replica_groups=mesh['row'=16,'col'=16] {'col'}, dimensions={0} | all-to-all | bytes 1048576 | tf_op jit(solution)/shard_map/all_to_all | solution.py:149
  291.7 1.9 reduce.1
  293.6 1.8 reshape.1302
  301.7 6.1 %all-to-all-start.7 = ((f32[2,1,1,512,128]{4,2,1,0,3:T(1,128)}), f32[2,1,1,512,128]{4,2,1,0,3:T(1,128)S(1)}, u32[]{:S(2)}, u32[]{:S(2)}) async-start(f32[2,1,1,512,128]{4,2,1,0,3:T(1,128)} %copy.372), calls=%async_computation.7 | async-start | bytes 1048576 | tf_op jit(solution)/shard_map/all_to_all | solution.py:152
  307.9 9.7 %all-to-all-done.7 = f32[2,1,1,512,128]{4,2,1,0,3:T(1,128)S(1)} async-done(((f32[2,1,1,512,128]{4,2,1,0,3:T(1,128)}), f32[2,1,1,512,128]{4,2,1,0,3:T(1,128)S(1)}, u32[]{:S(2)}, u32[]{:S(2)}) %all-to-all-start.7) | async-done | bytes 524320 | tf_op jit(solution)/shard_map/all_to_all | solution.py:152
  (197 shorter events, 86.8 us)
Async XLA Ops:
  5.2 16.6 %all-to-all-start = ((f32[2,1,16,32,128]{4,3,1,0,2:T(8,128)}), f32[2,1,16,32,128]{4,3,1,0,2:T(8,128)S(1)}, u32[]{:S(2)}, u32[]{:S(2)}) async-start(f32[2,1,16,32,128]{4,3,1,0,2:T(8,128)} %copy.316), calls=%async_computation | async-start | bytes 1048576 | tf_op jit(solution)/shard_map/all_to_all | solution.py:137
  27.1 27.3 %all-to-all-start.1 = ((f32[2,1,1,512,128]{4,2,1,0,3:T(1,128)}), f32[2,1,1,512,128]{4,2,1,0,3:T(1,128)S(1)}, u32[]{:S(2)}, u32[]{:S(2)}) async-start(f32[2,1,1,512,128]{4,2,1,0,3:T(1,128)} %pad_maximum_fusion.6), calls=%async_computation.1 | async-start | bytes 1048576 | tf_op jit(solution)/shard_map/all_to_all | solution.py:140
  38.0 21.9 %copy-start.17 = (f32[32]{0:T(128)}, f32[32]{0:T(128)S(1)}, u32[]{:S(2)}) copy-start(f32[32]{0:T(128)S(1)} %get-tuple-element.82) | copy-start | bytes 388
  38.7 21.2 %copy-start.20 = (f32[32]{0:T(128)}, f32[32]{0:T(128)S(1)}, u32[]{:S(2)}) copy-start(f32[32]{0:T(128)S(1)} %get-tuple-element.85) | copy-start | bytes 388
  76.8 4.1 %copy-start = (f32[2,1,32,32,64]{2,0,4,3,1:T(2,128)S(1)}, f32[2,1,32,32,64]{2,0,4,3,1:T(2,128)}, u32[]{:S(2)}) copy-start(f32[2,1,32,32,64]{2,0,4,3,1:T(2,128)} %copy.390) | copy-start | bytes 1572868
  86.1 11.1 %copy-start.22 = (f32[12]{0:T(128)S(1)}, f32[12]{0:T(128)}, u32[]{:S(2)}) copy-start(f32[12]{0:T(128)} %param.14) | copy-start | bytes 148
  86.1 11.1 %copy-start.23 = (f32[12]{0:T(128)S(1)}, f32[12]{0:T(128)}, u32[]{:S(2)}) copy-start(f32[12]{0:T(128)} %param.15) | copy-start | bytes 148
  86.1 12.5 %copy-start.7 = (s32[16,32,128]{2,1,0:T(8,128)S(1)}, s32[16,32,128]{2,1,0:T(8,128)}, u32[]{:S(2)}) copy-start(s32[16,32,128]{2,1,0:T(8,128)} %param.9) | copy-start | bytes 786436
  92.7 27.9 %copy-start.11 = (s32[4]{0:T(128)S(1)}, s32[4]{0:T(128)}, u32[]{:S(2)}) copy-start(s32[4]{0:T(128)} %param.17) | copy-start | bytes 52
  92.7 33.7 %copy-start.16 = (f32[33]{0:T(128)S(1)}, f32[33]{0:T(128)}, u32[]{:S(2)}) copy-start(f32[33]{0:T(128)} %param.16) | copy-start | bytes 400
  92.7 34.0 %all-to-all-start.2 = ((f32[16,1,16384]{2,1,0:T(1,128)}), f32[16,1,16384]{2,1,0:T(1,128)S(1)}, u32[]{:S(2)}, u32[]{:S(2)}) async-start(f32[16,1,16384]{2,1,0:T(1,128)} %reshape.1299), calls=%async_computation.2 | async-start | bytes 2097152 | tf_op jit(solution)/shard_map/all_to_all | solution.py:149
  115.4 40.2 %collective-permute-start = (f32[2,16,32,16]{3,2,1,0:T(8,128)}, f32[2,16,32,16]{3,2,1,0:T(8,128)}, u32[]{:S(2)}, u32[]{:S(2)}) collective-permute-start(f32[2,16,32,16]{3,2,1,0:T(8,128)} %get-tuple-element.48), channel_id=1, source_target_pairs={{0,1},{1,2},{2,3},{3,4},{4,5},{5,6},{6,7},{7,8},{8,9},{9,10},{10,1... | collective-permute-start | bytes 196616 | tf_op jit(solution)/shard_map/ppermute | solution.py:20
  118.3 37.3 %collective-permute-start.1 = (f32[2,16,32,16]{3,2,1,0:T(8,128)S(1)}, f32[2,16,32,16]{3,2,1,0:T(8,128)}, u32[]{:S(2)}, u32[]{:S(2)}) collective-permute-start(f32[2,16,32,16]{3,2,1,0:T(8,128)S(1)} %get-tuple-element.49), channel_id=1, source_target_pairs={{1,0},{2,1},{3,2},{4,3},{5,4},{6,5},{7,6},{8,7},{9,8},{10,9},{11,1... | collective-permute-start | bytes 196616 | tf_op jit(solution)/shard_map/ppermute | solution.py:21
  149.1 24.1 %all-to-all-start.3 = ((f32[2,2,1,512,128]{4,1,2,0,3:T(2,128)}), f32[2,2,1,512,128]{4,1,2,0,3:T(2,128)S(1)}, u32[]{:S(2)}, u32[]{:S(2)}) async-start(f32[2,2,1,512,128]{4,1,2,0,3:T(2,128)} %copy.337), calls=%async_computation.3 | async-start | bytes 2097152 | tf_op jit(solution)/shard_map/all_to_all | solution.py:152
  158.0 12.9 %collective-permute-start.2 = (f32[2,16,16,128]{3,2,1,0:T(8,128)S(1)}, f32[2,16,16,128]{3,2,1,0:T(8,128)S(1)}, u32[]{:S(2)}, u32[]{:S(2)}) collective-permute-start(f32[2,16,16,128]{3,2,1,0:T(8,128)S(1)} %get-tuple-element.46), channel_id=1, source_target_pairs={{0,16},{16,32},{32,48},{48,64},{64,80},{80,96},{96,112},{112,128},... | collective-permute-start | bytes 786440 | tf_op jit(solution)/shard_map/ppermute | solution.py:20
  159.7 12.8 %collective-permute-start.3 = (f32[2,16,16,128]{3,2,1,0:T(8,128)S(1)}, f32[2,16,16,128]{3,2,1,0:T(8,128)S(1)}, u32[]{:S(2)}, u32[]{:S(2)}) collective-permute-start(f32[2,16,16,128]{3,2,1,0:T(8,128)S(1)} %get-tuple-element.47), channel_id=1, source_target_pairs={{16,0},{32,16},{48,32},{64,48},{80,64},{96,80},{112,96},{128,112},... | collective-permute-start | bytes 786440 | tf_op jit(solution)/shard_map/ppermute | solution.py:21
  173.1 4.6 %copy-start.2 = (f32[2,16,32,128]{3,2,1,0:T(8,128)}, f32[2,16,32,128]{3,2,1,0:T(8,128)S(1)}, u32[]{:S(2)}) copy-start(f32[2,16,32,128]{3,2,1,0:T(8,128)S(1)} %convolution_bitcast_fusion) | copy-start | bytes 1572868
  175.3 2.5 copy-start.8
  175.3 2.5 copy-start.9
  175.4 2.5 copy-start.10
  175.4 2.5 copy-start.12
  175.4 2.5 copy-start.14
  178.1 3.0 copy-start.4
  178.1 3.0 copy-start.5
  178.1 3.0 copy-start.6
  211.3 33.4 %all-to-all-start.5 = ((f32[2,2,1,512,128]{4,1,2,0,3:T(2,128)}), f32[2,2,1,512,128]{4,1,2,0,3:T(2,128)S(1)}, u32[]{:S(2)}, u32[]{:S(2)}) async-start(f32[2,2,1,512,128]{4,1,2,0,3:T(2,128)} %pad_maximum_fusion.3), calls=%async_computation.5 | async-start | bytes 2097152 | tf_op jit(solution)/shard_map/all_to_all | solution.py:140
  255.4 1.2 copy-start.18
  299.1 8.8 %copy-start.13 = (f32[32]{0:T(128)S(1)}, f32[32]{0:T(128)}, u32[]{:S(2)}) copy-start(f32[32]{0:T(128)} %multiply_exponential_fusion) | copy-start | bytes 388
  299.1 8.8 %copy-start.15 = (f32[128]{0:T(128)S(1)}, f32[128]{0:T(128)}, u32[]{:S(2)}) copy-start(f32[128]{0:T(128)} %multiply_exponential_fusion.1) | copy-start | bytes 1540
  300.4 18.7 %copy-start.1 = (f32[16,32,128]{2,1,0:T(8,128)S(1)}, f32[16,32,128]{2,1,0:T(8,128)}, u32[]{:S(2)}) copy-start(f32[16,32,128]{2,1,0:T(8,128)} %param.10) | copy-start | bytes 786436
  300.4 18.7 %copy-start.3 = (f32[2,16,32,128]{3,2,1,0:T(8,128)S(1)}, f32[2,16,32,128]{3,2,1,0:T(8,128)}, u32[]{:S(2)}) copy-start(f32[2,16,32,128]{3,2,1,0:T(8,128)} %copy-done.2) | copy-start | bytes 1572868
  301.7 15.9 %all-to-all-start.7 = ((f32[2,1,1,512,128]{4,2,1,0,3:T(1,128)}), f32[2,1,1,512,128]{4,2,1,0,3:T(1,128)S(1)}, u32[]{:S(2)}, u32[]{:S(2)}) async-start(f32[2,1,1,512,128]{4,2,1,0,3:T(1,128)} %copy.372), calls=%async_computation.7 | async-start | bytes 1048576 | tf_op jit(solution)/shard_map/all_to_all | solution.py:152
  (2 other events, 2.4 us)
where the time goes:
time: 326 us; the launch traced here: 320 us
  waiting for transfers between devices  71.5 us (22%)
  matrix products  66.5 us (20%)
  starting transfers between devices  49.2 us (15%)
  blocking collectives  45.2 us (14%)
  local copies, waits for them, and re-layouts  44 us (13%)
  other arithmetic  37.5 us (12%)
  between operations  6.28 us (2%)
    dot_general x78, matrix products, product(): return jnp.einsum(form, operand, matrix, precision=highest)  63.5 us
    all_to_all x2, waiting for transfers between devices, forward_rows(): lax.all_to_all(stacked, 'col', split_axis=3, concat_axis=4, tiled=True)  41.3 us
    all_to_all x1, blocking collectives, inverse_rows(): lax.all_to_all(stacked, 'col', split_axis=4, concat_axis=3, tiled=True)  24.5 us
    all_to_all x1, blocking collectives, forward_rows(): lax.all_to_all(stacked, 'row', split_axis=2, concat_axis=3, tiled=True)  20.8 us
    all_to_all x2, starting transfers between devices, forward_rows(): lax.all_to_all(stacked, 'col', split_axis=3, concat_axis=4, tiled=True)  18.1 us
    another operation x3, other arithmetic, on_device(): coefficients = jnp.stack([buoyancy, modulus])  16.8 us
    unnamed x55, local copies, waits for them, and re-layouts  15.8 us
    all_to_all x2, starting transfers between devices, inverse_rows(): lax.all_to_all(stacked, 'row', split_axis=3, concat_axis=2, tiled=True)  12.6 us
  transfers between devices with their start and end apart: 10, of which 6 were waited for; matrix products, arithmetic and copies ran while one was open for 15% of the time, Pallas kernels for 0%

commit v1 on v0

--- a/solution.py
+++ b/solution.py
@@ -149,7 +149,13 @@
         untransform_y, lax.all_to_all(stacked, "col", split_axis=4, concat_axis=3, tiled=True)
     )
     stacked = packed(
-        depth_inverse, lax.all_to_all(stacked, "row", split_axis=3, concat_axis=2, tiled=True)
+        depth_inverse,
+        jnp.concatenate(
+            lax.all_to_all(
+                jnp.stack(jnp.split(stacked, lax.axis_size("row"), axis=3)), "row", 0, 0
+            ),
+            axis=2,
+        ),
     )
     return (stacked[0], stacked[1])
 

time: 326 us -> 342 us (1.049)
  local copies, waits for them, and re-layouts: 44 us -> 59.4 us
    unnamed x55 -> x83, local copies, waits for them, and re-layouts: 15.8 us -> 34 us
  transfers between devices with their start and end apart: 10 -> 10, of which waited for: 6 -> 6; matrix products, arithmetic and copies ran while one was open for 15% -> 17% of each run, Pallas kernels for 0% -> 0%
where the time goes in v1:
time: 342 us; the launch traced here: 336 us
  waiting for transfers between devices  71.4 us (21%)
  matrix products  65 us (19%)
  local copies, waits for them, and re-layouts  59.4 us (17%)
  starting transfers between devices  49.8 us (15%)
  blocking collectives  45 us (13%)
  other arithmetic  38.7 us (11%)
  between operations  6.24 us (2%)
    dot_general x78, matrix products, product(): return jnp.einsum(form, operand, matrix, precision=highest)  62.1 us
    all_to_all x2, waiting for transfers between devices, forward_rows(): lax.all_to_all(stacked, 'col', split_axis=3, concat_axis=4, tiled=True)  41.1 us
    unnamed x83, local copies, waits for them, and re-layouts  34 us
    all_to_all x1, blocking collectives, inverse_rows(): lax.all_to_all(stacked, 'col', split_axis=4, concat_axis=3, tiled=True)  24.4 us
    all_to_all x1, blocking collectives, forward_rows(): lax.all_to_all(stacked, 'row', split_axis=2, concat_axis=3, tiled=True)  20.6 us
    all_to_all x2, starting transfers between devices, forward_rows(): lax.all_to_all(stacked, 'col', split_axis=3, concat_axis=4, tiled=True)  18.4 us
    another operation x3, other arithmetic, on_device(): coefficients = jnp.stack([buoyancy, modulus])  16.9 us
    all_to_all x2, starting transfers between devices, inverse_rows(): lax.all_to_all(jnp.stack(jnp.split(stacked, lax.axis_size('row'), axis=3)...  12.8 us
  transfers between devices with their start and end apart: 10, of which 6 were waited for; matrix products, arithmetic and copies ran while one was open for 17% of the time, Pallas kernels for 0%

profile of v1, /device:TPU:1, one launch (start us, length us, event | category | flops | bytes accessed | tf_op | source)
XLA Modules:
  0.0 335.6 jit_solution(6054014276593848841)
XLA Ops:
  5.2 6.9 %all-to-all-start = ((f32[2,1,16,32,128]{4,3,1,0,2:T(8,128)}), f32[2,1,16,32,128]{4,3,1,0,2:T(8,128)S(1)}, u32[]{:S(2)}, u32[]{:S(2)}) async-start(f32[2,1,16,32,128]{4,3,1,0,2:T(8,128)} %copy.440), calls=%async_computation | async-start | bytes 1048576 | tf_op jit(solution)/shard_map/all_to_all | solution.py:137
  12.4 9.4 %all-to-all-done = f32[2,1,16,32,128]{4,3,1,0,2:T(8,128)S(1)} async-done(((f32[2,1,16,32,128]{4,3,1,0,2:T(8,128)}), f32[2,1,16,32,128]{4,3,1,0,2:T(8,128)S(1)}, u32[]{:S(2)}, u32[]{:S(2)}) %all-to-all-start) | async-done | bytes 524320 | tf_op jit(solution)/shard_map/all_to_all | solution.py:137
  27.2 10.6 %all-to-all-start.1 = ((f32[2,1,1,512,128]{4,2,1,0,3:T(1,128)}), f32[2,1,1,512,128]{4,2,1,0,3:T(1,128)S(1)}, u32[]{:S(2)}, u32[]{:S(2)}) async-start(f32[2,1,1,512,128]{4,2,1,0,3:T(1,128)} %pad_maximum_fusion.7), calls=%async_computation.1 | async-start | bytes 1048576 | tf_op jit(solution)/shard_map/all_to_all | solution.py:140
  39.0 15.5 %all-to-all-done.1 = f32[2,1,1,512,128]{4,2,1,0,3:T(1,128)S(1)} async-done(((f32[2,1,1,512,128]{4,2,1,0,3:T(1,128)}), f32[2,1,1,512,128]{4,2,1,0,3:T(1,128)S(1)}, u32[]{:S(2)}, u32[]{:S(2)}) %all-to-all-start.1) | async-done | bytes 524320 | tf_op jit(solution)/shard_map/all_to_all | solution.py:140
  59.9 1.8 add_bitcast_fusion.3
  68.5 2.1 fusion.5
  70.6 3.9 %copy.536 = f32[2,1,32,32,64]{2,0,4,3,1:T(2,128)} copy(f32[2,1,32,32,64]{4,3,2,0,1:T(8,128)} %fusion.5) | data formatting | bytes 1048576 | tf_op jit(solution)/shard_map/stack;reshape | solution.py:147
  74.5 2.1 fusion.3
  76.6 4.1 %copy.537 = f32[2,1,32,32,64]{2,0,4,3,1:T(2,128)} copy(f32[2,1,32,32,64]{4,3,2,0,1:T(8,128)} %fusion.3) | data formatting | bytes 1048576 | tf_op jit(solution)/shard_map/stack;reshape | solution.py:147
  80.7 5.2 %fusion.756 = f32[2048,2,1,2,32]{4,3,2,1,0:T(2,128)} fusion(f32[1,2,1,32,2048]{3,1,2,0,4:T(2,128)} %bitcast.746, f32[1,2,1,32,2048]{3,1,2,0,4:T(2,128)S(1)} %bitcast.745), kind=kLoop, calls=%fused_computation.920 | loop fusion | flops 262144 | bytes 2097152
  85.9 6.6 %reshape.1299 = f32[16,1,16384]{2,1,0:T(1,128)} reshape(f32[2048,2,1,2,32]{4,3,2,1,0:T(2,128)} %fusion.756) | data formatting | bytes 2097152
  92.5 4.5 %all-to-all-start.2 = ((f32[16,1,16384]{2,1,0:T(1,128)}), f32[16,1,16384]{2,1,0:T(1,128)S(1)}, u32[]{:S(2)}, u32[]{:S(2)}) async-start(f32[16,1,16384]{2,1,0:T(1,128)} %reshape.1299), calls=%async_computation.2 | async-start | bytes 2097152 | tf_op jit(solution)/shard_map/all_to_all | solution.py:149
  98.4 8.1 %select_bitcast_fusion.1 = (f32[1,16,32,128]{3,2,1,0:T(8,128)S(1)}, pred[16,32,128]{2,1,0:T(8,128)(4,1)S(1)}, pred[16,32,128]{2,1,0:T(8,128)(4,1)S(1)}, pred[16,...) fusion(f32[]{:T(128)} %bitcast.19, f32[]{:T(128)} %bitcast.18, ...), kind=kLoop, calls=%fused_computation.236 | loop fusion | flops 1572864 | bytes 1310768 | tf_op jit(solution)/shard_map/stack | solution.py:231
  106.5 7.8 %select_bitcast_fusion = f32[1,16,32,128]{3,2,1,0:T(8,128)S(1)} fusion(pred[16,32,128]{2,1,0:T(8,128)(4,1)S(1)} %get-tuple-element.16, pred[16,32,128]{2,1,0:T(8,128)(4,1)S(1)} %get-tuple-element.15, pred[16,32,128]{2,1,0:T(8,128)(4,1)S(1)} %get-tuple-element.14, pred[16,32,128]{2,1,0:T(8,128)(4,1)S(1)} %get-tuple-element.13, ...), kind=kLoop, calls=%fused_computation.235 | loop fusion | flops 786432 | bytes 1048624 | tf_op jit(solution)/shard_map/stack | solution.py:231
  115.3 2.9 collective-permute-start
  118.2 2.6 collective-permute-start.1
  127.4 3.1 reduce
  130.6 4.9 %reshape.1300 = f32[2048,2,1,2,32]{4,3,2,1,0:T(2,128)} reshape(f32[16,16384]{1,0:T(8,128)S(1)} %reduce) | data formatting | bytes 2097152
  135.5 5.2 %copy.454 = f32[2,2,1,32,16,128]{5,3,4,1,2,0:T(8,128)S(1)} copy(f32[2,2,1,32,16,128]{3,1,0,5,4,2:T(2,128)} %bitcast.734) | data formatting | bytes 2097152 | tf_op jit(solution)/shard_map/all_to_all | solution.py:149
  157.3 6.7 %all-to-all-start.3 = ((f32[16,2,2,1,32,128]{5,4,2,3,1,0:T(8,128)}), f32[16,2,2,1,32,128]{5,4,2,3,1,0:T(8,128)S(1)}, u32[]{:S(2)}, u32[]{:S(2)}) async-start(f32[16,2,2,1,32,128]{5,4,2,3,1,0:T(8,128)} %bitcast.150), calls=%async_computation.3 | async-start | bytes 2097152 | tf_op jit(solution)/shard_map/all_to_all | solution.py:154
  164.1 2.3 fusion.29
  166.5 1.7 collective-permute-start.2
  169.6 9.7 %collective-permute-done.2 = f32[2,16,16,128]{3,2,1,0:T(8,128)S(1)} collective-permute-done((f32[2,16,16,128]{3,2,1,0:T(8,128)S(1)}, f32[2,16,16,128]{3,2,1,0:T(8,128)S(1)}, u32[]{:S(2)}, u32[]{:S(2)}) %collective-permute-start.2) | collective-permute-done | bytes 262176 | tf_op jit(solution)/shard_map/ppermute | solution.py:20
  189.1 20.6 %all_to_all.88 = f32[2,2,16,32,128]{4,3,1,0,2:T(8,128)S(1)} all-to-all(f32[2,2,16,32,128]{4,3,1,0,2:T(8,128)S(1)} %copy.486), channel_id=1, replica_groups=mesh['row'=16,'col'=16] {'row'}, dimensions={2} | all-to-all | bytes 2097152 | tf_op jit(solution)/shard_map/all_to_all | solution.py:137
  218.6 7.8 %all-to-all-start.5 = ((f32[2,2,1,512,128]{4,1,2,0,3:T(2,128)}), f32[2,2,1,512,128]{4,1,2,0,3:T(2,128)S(1)}, u32[]{:S(2)}, u32[]{:S(2)}) async-start(f32[2,2,1,512,128]{4,1,2,0,3:T(2,128)} %pad_maximum_fusion.3), calls=%async_computation.5 | async-start | bytes 2097152 | tf_op jit(solution)/shard_map/all_to_all | solution.py:140
  226.4 25.7 %all-to-all-done.5 = f32[2,2,1,512,128]{4,1,2,0,3:T(2,128)S(1)} async-done(((f32[2,2,1,512,128]{4,1,2,0,3:T(2,128)}), f32[2,2,1,512,128]{4,1,2,0,3:T(2,128)S(1)}, u32[]{:S(2)}, u32[]{:S(2)}) %all-to-all-start.5) | async-done | bytes 1048608 | tf_op jit(solution)/shard_map/all_to_all | solution.py:140
  272.5 2.0 reshape.1301
  274.5 24.4 %all_to_all.89 = f32[16,1,8192]{2,1,0:T(1,128)S(1)} all-to-all(f32[16,1,8192]{2,1,0:T(1,128)S(1)} %reshape.1301), channel_id=1, replica_groups=mesh['row'=16,'col'=16] {'col'}, dimensions={0} | all-to-all | bytes 1048576 | tf_op jit(solution)/shard_map/all_to_all | solution.py:149
  299.0 1.9 reduce.1
  300.9 1.8 reshape.1302
  317.4 6.1 %all-to-all-start.7 = ((f32[16,2,1,1,32,128]{5,4,3,2,1,0:T(8,128)}), f32[16,2,1,1,32,128]{5,4,3,2,1,0:T(8,128)S(1)}, u32[]{:S(2)}, u32[]{:S(2)}) async-start(f32[16,2,1,1,32,128]{5,4,3,2,1,0:T(8,128)} %bitcast.258), calls=%async_computation.7 | async-start | bytes 1048576 | tf_op jit(solution)/shard_map/all_to_all | solution.py:154
  323.6 9.7 %all-to-all-done.7 = f32[16,2,1,1,32,128]{5,4,3,2,1,0:T(8,128)S(1)} async-done(((f32[16,2,1,1,32,128]{5,4,3,2,1,0:T(8,128)}), f32[16,2,1,1,32,128]{5,4,3,2,1,0:T(8,128)S(1)}, u32[]{:S(2)}, u32[]{:S(2)}) %all-to-all-start.7) | async-done | bytes 524320 | tf_op jit(solution)/shard_map/all_to_all | solution.py:154
  (225 shorter events, 101.8 us)
Async XLA Ops:
  5.2 16.6 %all-to-all-start = ((f32[2,1,16,32,128]{4,3,1,0,2:T(8,128)}), f32[2,1,16,32,128]{4,3,1,0,2:T(8,128)S(1)}, u32[]{:S(2)}, u32[]{:S(2)}) async-start(f32[2,1,16,32,128]{4,3,1,0,2:T(8,128)} %copy.440), calls=%async_computation | async-start | bytes 1048576 | tf_op jit(solution)/shard_map/all_to_all | solution.py:137
  27.2 27.3 %all-to-all-start.1 = ((f32[2,1,1,512,128]{4,2,1,0,3:T(1,128)}), f32[2,1,1,512,128]{4,2,1,0,3:T(1,128)S(1)}, u32[]{:S(2)}, u32[]{:S(2)}) async-start(f32[2,1,1,512,128]{4,2,1,0,3:T(1,128)} %pad_maximum_fusion.7), calls=%async_computation.1 | async-start | bytes 1048576 | tf_op jit(solution)/shard_map/all_to_all | solution.py:140
  38.0 21.9 %copy-start.17 = (f32[32]{0:T(128)}, f32[32]{0:T(128)S(1)}, u32[]{:S(2)}) copy-start(f32[32]{0:T(128)S(1)} %get-tuple-element.78) | copy-start | bytes 388
  38.6 21.3 %copy-start.20 = (f32[32]{0:T(128)}, f32[32]{0:T(128)S(1)}, u32[]{:S(2)}) copy-start(f32[32]{0:T(128)S(1)} %get-tuple-element.81) | copy-start | bytes 388
  76.6 4.1 %copy-start = (f32[2,1,32,32,64]{2,0,4,3,1:T(2,128)S(1)}, f32[2,1,32,32,64]{2,0,4,3,1:T(2,128)}, u32[]{:S(2)}) copy-start(f32[2,1,32,32,64]{2,0,4,3,1:T(2,128)} %copy.536) | copy-start | bytes 1572868
  85.9 11.1 %copy-start.22 = (f32[12]{0:T(128)S(1)}, f32[12]{0:T(128)}, u32[]{:S(2)}) copy-start(f32[12]{0:T(128)} %param.14) | copy-start | bytes 148
  85.9 11.1 %copy-start.23 = (f32[12]{0:T(128)S(1)}, f32[12]{0:T(128)}, u32[]{:S(2)}) copy-start(f32[12]{0:T(128)} %param.15) | copy-start | bytes 148
  85.9 12.6 %copy-start.7 = (s32[16,32,128]{2,1,0:T(8,128)S(1)}, s32[16,32,128]{2,1,0:T(8,128)}, u32[]{:S(2)}) copy-start(s32[16,32,128]{2,1,0:T(8,128)} %param.9) | copy-start | bytes 786436
  92.5 28.3 %copy-start.11 = (s32[4]{0:T(128)S(1)}, s32[4]{0:T(128)}, u32[]{:S(2)}) copy-start(s32[4]{0:T(128)} %param.17) | copy-start | bytes 52
  92.5 34.1 %copy-start.16 = (f32[33]{0:T(128)S(1)}, f32[33]{0:T(128)}, u32[]{:S(2)}) copy-start(f32[33]{0:T(128)} %param.16) | copy-start | bytes 400
  92.5 34.4 %all-to-all-start.2 = ((f32[16,1,16384]{2,1,0:T(1,128)}), f32[16,1,16384]{2,1,0:T(1,128)S(1)}, u32[]{:S(2)}, u32[]{:S(2)}) async-start(f32[16,1,16384]{2,1,0:T(1,128)} %reshape.1299), calls=%async_computation.2 | async-start | bytes 2097152 | tf_op jit(solution)/shard_map/all_to_all | solution.py:149
  115.3 48.7 %collective-permute-start = (f32[2,16,32,16]{3,2,1,0:T(8,128)}, f32[2,16,32,16]{3,2,1,0:T(8,128)}, u32[]{:S(2)}, u32[]{:S(2)}) collective-permute-start(f32[2,16,32,16]{3,2,1,0:T(8,128)} %get-tuple-element.44), channel_id=1, source_target_pairs={{0,1},{1,2},{2,3},{3,4},{4,5},{5,6},{6,7},{7,8},{8,9},{9,10},{10,1... | collective-permute-start | bytes 196616 | tf_op jit(solution)/shard_map/ppermute | solution.py:20
  118.2 45.9 %collective-permute-start.1 = (f32[2,16,32,16]{3,2,1,0:T(8,128)S(1)}, f32[2,16,32,16]{3,2,1,0:T(8,128)}, u32[]{:S(2)}, u32[]{:S(2)}) collective-permute-start(f32[2,16,32,16]{3,2,1,0:T(8,128)S(1)} %get-tuple-element.45), channel_id=1, source_target_pairs={{1,0},{2,1},{3,2},{4,3},{5,4},{6,5},{7,6},{8,7},{9,8},{10,9},{11,1... | collective-permute-start | bytes 196616 | tf_op jit(solution)/shard_map/ppermute | solution.py:21
  157.3 24.2 %all-to-all-start.3 = ((f32[16,2,2,1,32,128]{5,4,2,3,1,0:T(8,128)}), f32[16,2,2,1,32,128]{5,4,2,3,1,0:T(8,128)S(1)}, u32[]{:S(2)}, u32[]{:S(2)}) async-start(f32[16,2,2,1,32,128]{5,4,2,3,1,0:T(8,128)} %bitcast.150), calls=%async_computation.3 | async-start | bytes 2097152 | tf_op jit(solution)/shard_map/all_to_all | solution.py:154
  166.5 12.8 %collective-permute-start.2 = (f32[2,16,16,128]{3,2,1,0:T(8,128)S(1)}, f32[2,16,16,128]{3,2,1,0:T(8,128)S(1)}, u32[]{:S(2)}, u32[]{:S(2)}) collective-permute-start(f32[2,16,16,128]{3,2,1,0:T(8,128)S(1)} %get-tuple-element.42), channel_id=1, source_target_pairs={{0,16},{16,32},{32,48},{48,64},{64,80},{80,96},{96,112},{112,128},... | collective-permute-start | bytes 786440 | tf_op jit(solution)/shard_map/ppermute | solution.py:20
  168.2 12.6 %collective-permute-start.3 = (f32[2,16,16,128]{3,2,1,0:T(8,128)S(1)}, f32[2,16,16,128]{3,2,1,0:T(8,128)S(1)}, u32[]{:S(2)}, u32[]{:S(2)}) collective-permute-start(f32[2,16,16,128]{3,2,1,0:T(8,128)S(1)} %get-tuple-element.43), channel_id=1, source_target_pairs={{16,0},{32,16},{48,32},{64,48},{80,64},{96,80},{112,96},{128,112},... | collective-permute-start | bytes 786440 | tf_op jit(solution)/shard_map/ppermute | solution.py:21
  181.5 3.8 %copy-start.2 = (f32[2,16,32,128]{3,2,1,0:T(8,128)}, f32[2,16,32,128]{3,2,1,0:T(8,128)S(1)}, u32[]{:S(2)}) copy-start(f32[2,16,32,128]{3,2,1,0:T(8,128)S(1)} %convolution_bitcast_fusion) | copy-start | bytes 1572868
  183.3 2.0 copy-start.8
  183.3 2.0 copy-start.9
  183.4 2.0 copy-start.10
  183.4 2.0 copy-start.12
  183.4 2.0 copy-start.14
  185.6 3.0 copy-start.4
  185.6 3.0 copy-start.5
  185.6 3.0 copy-start.6
  218.6 33.4 %all-to-all-start.5 = ((f32[2,2,1,512,128]{4,1,2,0,3:T(2,128)}), f32[2,2,1,512,128]{4,1,2,0,3:T(2,128)S(1)}, u32[]{:S(2)}, u32[]{:S(2)}) async-start(f32[2,2,1,512,128]{4,1,2,0,3:T(2,128)} %pad_maximum_fusion.3), calls=%async_computation.5 | async-start | bytes 2097152 | tf_op jit(solution)/shard_map/all_to_all | solution.py:140
  262.8 1.2 copy-start.18
  306.9 16.6 %copy-start.13 = (f32[32]{0:T(128)S(1)}, f32[32]{0:T(128)}, u32[]{:S(2)}) copy-start(f32[32]{0:T(128)} %multiply_exponential_fusion) | copy-start | bytes 388
  306.9 16.6 %copy-start.15 = (f32[128]{0:T(128)S(1)}, f32[128]{0:T(128)}, u32[]{:S(2)}) copy-start(f32[128]{0:T(128)} %multiply_exponential_fusion.1) | copy-start | bytes 1540
  307.6 26.8 %copy-start.1 = (f32[16,32,128]{2,1,0:T(8,128)S(1)}, f32[16,32,128]{2,1,0:T(8,128)}, u32[]{:S(2)}) copy-start(f32[16,32,128]{2,1,0:T(8,128)} %param.10) | copy-start | bytes 786436
  307.7 26.8 %copy-start.3 = (f32[2,16,32,128]{3,2,1,0:T(8,128)S(1)}, f32[2,16,32,128]{3,2,1,0:T(8,128)}, u32[]{:S(2)}) copy-start(f32[2,16,32,128]{3,2,1,0:T(8,128)} %copy-done.2) | copy-start | bytes 1572868
  317.4 15.9 %all-to-all-start.7 = ((f32[16,2,1,1,32,128]{5,4,3,2,1,0:T(8,128)}), f32[16,2,1,1,32,128]{5,4,3,2,1,0:T(8,128)S(1)}, u32[]{:S(2)}, u32[]{:S(2)}) async-start(f32[16,2,1,1,32,128]{5,4,3,2,1,0:T(8,128)} %bitcast.258), calls=%async_computation.7 | async-start | bytes 1048576 | tf_op jit(solution)/shard_map/all_to_all | solution.py:154
  (2 other events, 2.4 us)
